TPU v7x, 32 devices: a whole 2x2x4 slice. The times are simulated.
32 devices in a mesh: node: 16 (over z, x, core), col: 2 (over y).
Axes of the slice: x: 2, y: 2, z: 4, core: 2. Of those that a mesh axis runs over, the one named last changes fastest.
Arguments:
- coefficients: bfloat16 [64, 256, 2048], P('node', None, 'col'), may hold values from -6 to 6
- transfer: bfloat16 [3, 64, 4, 256, 256], P(None, 'node', None, 'col'), may hold values from -0.1875 to 0.1875
Outputs:
- result: bfloat16 [64, 256, 2048], P('node', None, 'col')
All inputs are finite; a program needn't handle non-finite values.
Results may differ from a plain program's by a relative error of at most 0.0058.
Values may be sent and summed in bfloat16 or wider, within the bound.
A program may use at most 64 MiB of HBM per device.

v0:
```python
import functools

import jax
import jax.numpy as jnp
from jax import lax
from jax.experimental import pallas as pl
from jax.experimental.pallas import tpu as pltpu
from jax.sharding import PartitionSpec as P

MESH = pl.DeviceIdType.MESH
WIDTH = 256
LAG_FORWARD, LAG_ONE, LAG_RELAY, LAG_FAR, LAG_MID, LAG_END = 2, 4, 7, 5, 9, 11
TO_CORE, TO_TWO, FORWARD, TO_PAIR, TO_ACROSS, RELAY, PARTIAL = range(7)


def flip(i, bit):
    return i + bit - 2 * bit * (i // bit % 2)


def dot(a, b):
    return jnp.dot(a, b, preferred_element_type=jnp.float32)


def kernel(
    cols, chunks, x_in, t_in, out_ref,
    x, t, t_far, y0, near, y1, pair, across, relayed, partial_out, partial_in, out_buf,
    x_sem, t_sem, out_sem, send, recv, t_send, t_recv, far_send, far_recv,
):
    nodes_here = x_in.shape[0]
    rows = t_in.shape[3]
    units = nodes_here * chunks
    width = x_in.shape[2] // chunks
    me = lax.axis_index("node")
    my_col = lax.axis_index("col")
    one = me % 4
    two = me // 4 % 4
    is_mid = (two + 1) // 2 % 2 == 1
    is_end = (two + 1) // 2 % 2 == 0
    by_core, by_two, by_pair = flip(me, 1), flip(me, 2), flip(me, 4)
    by_across = flip(flip(me, 4), 8)

    x_copy = pltpu.make_async_copy(x_in, x, x_sem)
    x_copy.start()
    t_copy = pltpu.make_async_copy(t_in, t.at[:, :, :, pl.ds(my_col * rows, rows), :], t_sem)
    t_copy.start()

    barrier = pltpu.get_barrier_semaphore()
    for other in (by_core, by_two, by_pair):
        pl.semaphore_signal(barrier, inc=1, device_id={"node": other}, device_id_type=MESH)
    for k in range(1, cols):
        pl.semaphore_signal(barrier, inc=1, device_id={"col": (my_col + k) % cols}, device_id_type=MESH)

    @pl.when(is_mid)
    def _():
        pl.semaphore_signal(barrier, inc=1, device_id={"node": by_across}, device_id_type=MESH)
        pl.semaphore_wait(barrier, 4 + cols - 1)

    @pl.when(is_end)
    def _():
        pl.semaphore_wait(barrier, 3 + cols - 1)

    def t_rows(level, m, k):
        return pltpu.make_async_remote_copy(
            src_ref=t_in.at[level, m],
            dst_ref=t.at[level, m, :, pl.ds(my_col * rows, rows), :],
            send_sem=t_send.at[level, m, k - 1],
            recv_sem=t_recv.at[level, m, k - 1],
            device_id={"col": (my_col + k) % cols},
            device_id_type=MESH,
        )

    def wait_rows(level, m):
        for k in range(1, cols):
            source = (my_col + cols - k) % cols
            pltpu.make_async_remote_copy(
                src_ref=t_in.at[level, m],
                dst_ref=t.at[level, m, :, pl.ds(source * rows, rows), :],
                send_sem=t_send.at[level, m, k - 1],
                recv_sem=t_recv.at[level, m, k - 1],
                device_id={"col": (my_col + k) % cols},
                device_id_type=MESH,
            ).wait_recv()

    order = sorted((2 * m + (0, 1, 3)[level], level, m) for m in range(nodes_here) for level in range(3))
    for _, level, m in order:
        for k in range(1, cols):
            t_rows(level, m, k).start()

    routes = {
        TO_CORE: (y0, near.at[0], by_core),
        TO_TWO: (y0, near.at[1], by_two),
        FORWARD: (near.at[1], near.at[2], by_core),
        TO_PAIR: (y1, pair, by_pair),
        TO_ACROSS: (y1, across, by_across),
        RELAY: (pair, relayed, by_across),
        PARTIAL: (partial_out, partial_in, by_pair),
    }

    def copy(kind, u):
        source, target, device = routes[kind]
        return pltpu.make_async_remote_copy(
            src_ref=source.at[u],
            dst_ref=target.at[u],
            send_sem=send.at[kind, u],
            recv_sem=recv.at[kind, u],
            device_id={"node": device},
            device_id_type=MESH,
        )

    def far(m, i):
        return pltpu.make_async_remote_copy(
            src_ref=t.at[2, m, flip(two, 2) if i == 0 else 3 - two],
            dst_ref=t_far.at[m, i],
            send_sem=far_send.at[m, i],
            recv_sem=far_recv.at[m, i],
            device_id={"node": by_pair},
            device_id_type=MESH,
        )

    def out_copy(u):
        columns = pl.ds(pl.multiple_of(u % chunks * width, width), width)
        return pltpu.make_async_copy(out_buf.at[u], out_ref.at[u // chunks, :, columns], out_sem.at[u])

    def first(u, action):
        @pl.when(u % chunks == 0)
        def _():
            action(u // chunks)

    def stage_zero(u):
        first(u, lambda m: wait_rows(0, m))
        m = u // chunks
        columns = pl.ds(pl.multiple_of(u % chunks * width, width), width)
        total = dot(t[0, m, 0], x[0, :, columns])
        for j in range(1, 4):
            total += dot(t[0, m, j], x[j, :, columns])
        y0[u] = total.astype(y0.dtype)
        copy(TO_TWO, u).start()
        copy(TO_CORE, u).start()

    def stage_forward(u):
        copy(TO_TWO, u).wait_recv()
        copy(FORWARD, u).start()

    def stage_one(u):
        first(u, lambda m: wait_rows(1, m))
        m = u // chunks
        copy(TO_CORE, u).wait_recv()
        copy(FORWARD, u).wait_recv()
        total = dot(t[1, m, one], y0[u])
        total += dot(t[1, m, flip(one, 1)], near[0, u])
        total += dot(t[1, m, flip(one, 2)], near[1, u])
        total += dot(t[1, m, 3 - one], near[2, u])
        y1[u] = total.astype(y1.dtype)

        @pl.when(is_mid)
        def _():
            copy(TO_ACROSS, u).start()

        copy(TO_PAIR, u).start()

    def stage_relay(u):
        copy(TO_PAIR, u).wait_recv()
        copy(RELAY, u).start()

    def stage_far(u):
        def send_far(m):
            wait_rows(2, m)
            far(m, 0).start()
            far(m, 1).start()

        first(u, send_far)

    def stage_mid(u):
        def arrive(m):
            wait_rows(2, m)
            far(m, 0).wait_recv()
            far(m, 1).wait_recv()

        first(u, arrive)
        m = u // chunks
        copy(TO_ACROSS, u).wait_recv()
        copy(RELAY, u).wait_recv()
        part = dot(t_far[m, 0], across[u]) + dot(t_far[m, 1], relayed[u])
        partial_out[u] = part.astype(partial_out.dtype)
        copy(PARTIAL, u).start()
        total = dot(t[2, m, two], y1[u])
        total += dot(t[2, m, flip(two, 1)], pair[u])
        total += dot(t[2, m, 3 - two], across[u])
        total += dot(t[2, m, flip(two, 2)], relayed[u])
        out_buf[u] = total.astype(out_buf.dtype)
        out_copy(u).start()

    def stage_end(u):
        m = u // chunks
        copy(TO_PAIR, u).wait_recv()
        total = dot(t[2, m, two], y1[u]) + dot(t[2, m, flip(two, 1)], pair[u])
        copy(PARTIAL, u).wait_recv()
        out_buf[u] = (total + partial_in[u].astype(jnp.float32)).astype(out_buf.dtype)
        out_copy(u).start()

    x_copy.wait()
    t_copy.wait()

    def step(s, _):
        def run(stage, lag, role=None):
            u = s - lag
            ready = (u >= 0) & (u < units)

            @pl.when(ready if role is None else ready & role)
            def _():
                stage(u)

        run(stage_forward, LAG_FORWARD)
        run(stage_one, LAG_ONE)
        run(stage_relay, LAG_RELAY, is_mid)
        run(stage_far, LAG_FAR, is_end)
        run(stage_mid, LAG_MID, is_mid)
        run(stage_end, LAG_END, is_end)
        run(stage_zero, 0)
        return 0

    lax.fori_loop(0, units + LAG_END, step, 0)

    def drain(u, _):
        for kind in (TO_CORE, TO_TWO, FORWARD, TO_PAIR):
            copy(kind, u).wait_send()

        @pl.when(is_mid)
        def _():
            for kind in (TO_ACROSS, RELAY, PARTIAL):
                copy(kind, u).wait_send()

        out_copy(u).wait()
        return 0

    lax.fori_loop(0, units, drain, 0)

    def drain_rows(m, _):
        for level in range(3):
            for k in range(1, cols):
                t_rows(level, m, k).wait_send()

        @pl.when(is_end)
        def _():
            far(m, 0).wait_send()
            far(m, 1).wait_send()

        return 0

    lax.fori_loop(0, nodes_here, drain_rows, 0)


def local(coefficients, transfer):
    cols = lax.axis_size("col")
    nodes_here, rank, columns = coefficients.shape
    levels, _, children, rows, _ = transfer.shape
    width = min(WIDTH, columns)
    chunks = columns // width
    units = nodes_here * chunks
    kind = coefficients.dtype
    block = (units, rank, width)
    return pl.pallas_call(
        functools.partial(kernel, cols, chunks),
        out_shape=jax.ShapeDtypeStruct(coefficients.shape, kind),
        in_specs=[pl.BlockSpec(memory_space=pl.ANY)] * 2,
        out_specs=pl.BlockSpec(memory_space=pl.ANY),
        scratch_shapes=[
            pltpu.VMEM(coefficients.shape, kind),
            pltpu.VMEM((levels, nodes_here, children, rank, rank), kind),
            pltpu.VMEM((nodes_here, 2, rank, rank), kind),
            pltpu.VMEM(block, kind),
            pltpu.VMEM((3,) + block, kind),
            pltpu.VMEM(block, kind),
            pltpu.VMEM(block, kind),
            pltpu.VMEM(block, kind),
            pltpu.VMEM(block, kind),
            pltpu.VMEM(block, kind),
            pltpu.VMEM(block, kind),
            pltpu.VMEM(block, kind),
            pltpu.SemaphoreType.DMA,
            pltpu.SemaphoreType.DMA,
            pltpu.SemaphoreType.DMA((units,)),
            pltpu.SemaphoreType.DMA((7, units)),
            pltpu.SemaphoreType.DMA((7, units)),
            pltpu.SemaphoreType.DMA((levels, nodes_here, max(cols - 1, 1))),
            pltpu.SemaphoreType.DMA((levels, nodes_here, max(cols - 1, 1))),
            pltpu.SemaphoreType.DMA((nodes_here, 2)),
            pltpu.SemaphoreType.DMA((nodes_here, 2)),
        ],
        compiler_params=pltpu.CompilerParams(
            collective_id=0, has_side_effects=True, vmem_limit_bytes=56 * 1024 * 1024
        ),
    )(coefficients, transfer)


def solution(mesh):
    return jax.shard_map(
        local,
        mesh=mesh,
        in_specs=(P("node", None, "col"), P(None, "node", None, "col", None)),
        out_specs=P("node", None, "col"),
        check_vma=False,
    )
```

profile of v0, /device:TPU:0, one launch (start us, length us, event | category | flops | bytes accessed | tf_op | source)
XLA Modules:
  0.0 124.7 jit_solution(8072542554705483676)
XLA Ops:
  0.0 121.6 %shard_map.28 = bf16[4,256,1024]{2,1,0:T(8,128)(2,1)} custom-call(bf16[4,256,1024]{2,1,0:T(8,128)(2,1)} %x_in.1, bf16[3,4,4,128,256]{4,3,2,1,0:T(8,128)(2,1)} %t_in.1), custom_call_target="tpu_custom_call" | custom-call | tf_op jit(solution)/shard_map/pallas_call | solution.py:262
  121.6 3.1 %copy.4 = bf16[4,256,1024]{2,1,0:T(8,128)(2,1)} copy(bf16[4,256,1024]{2,1,0:T(8,128)(2,1)} %shard_map.28) | data formatting | bytes 4194304
where the time goes:
time: 125 us
  Pallas kernels  122 us (98%)
  local copies, waits for them, and re-layouts  3.08 us (2%)
    pallas_call x1, Pallas kernels, local(): pl.pallas_call(functools.partial(kernel, cols, chunks), out_shape=jax.Sha...  122 us
    unnamed x1, local copies, waits for them, and re-layouts  3.08 us

commit v1 on v0

v1 whole, which is shorter than its diff:
```python
import functools

import jax
import jax.numpy as jnp
from jax import lax
from jax.experimental import pallas as pl
from jax.experimental.pallas import tpu as pltpu
from jax.sharding import PartitionSpec as P

MESH = pl.DeviceIdType.MESH
WIDTH = 256
LAG_ONE, LAG_RELAY, LAG_FAR, LAG_MID, LAG_END = 3, 5, 8, 11, 13
TO_TWO, FORWARD, TO_PAIR, TO_ACROSS, RELAY, PARTIAL, SUM_NEAR, SUM_FAR = range(8)
ROW = {TO_TWO: 0, FORWARD: 1, TO_PAIR: 2, TO_ACROSS: 3, RELAY: 4, PARTIAL: 3, SUM_NEAR: 3, SUM_FAR: 3}


def flip(i, bit):
    return i + bit - 2 * bit * (i // bit % 2)


def dot(a, b):
    return jnp.dot(a, b, preferred_element_type=jnp.float32)


def kernel(
    cols, chunks, x_in, t_in, out_ref,
    x, t, t_far, t_sum, held, theirs, y1, pair, across, relayed, partial_out, partial_in, sums,
    local_sem, send, recv, t_send, t_recv, far_send, far_recv, sum_send, sum_recv, spread_send, spread_recv,
):
    nodes_here = x_in.shape[0]
    last = nodes_here - 1
    rows = t_in.shape[3]
    units = nodes_here * chunks
    plain = last * chunks
    width = x_in.shape[2] // chunks
    me = lax.axis_index("node")
    my_col = lax.axis_index("col")
    one = me % 4
    two = me // 4 % 4
    side = two // 2 * 2
    other = 2 - side
    is_mid = (two + 1) // 2 % 2 == 1
    is_end = (two + 1) // 2 % 2 == 0
    by_core, by_two, by_pair, by_cross = flip(me, 1), flip(me, 2), flip(me, 4), flip(me, 8)
    by_across = flip(by_pair, 8)
    my_rows = pl.ds(my_col * rows, rows)

    x_copy = pltpu.make_async_copy(x_in, x, local_sem.at[0])
    x_copy.start()
    t_copy = pltpu.make_async_copy(t_in, t.at[:, :, :, my_rows, :], local_sem.at[1])
    t_copy.start()

    barrier = pltpu.get_barrier_semaphore()
    for k in range(1, cols):
        pl.semaphore_signal(barrier, inc=1, device_id={"col": (my_col + k) % cols}, device_id_type=MESH)
    for device in (by_cross, by_pair, by_two, by_core):
        pl.semaphore_signal(barrier, inc=1, device_id={"node": device}, device_id_type=MESH)

    @pl.when(is_mid)
    def _():
        pl.semaphore_signal(barrier, inc=1, device_id={"node": by_across}, device_id_type=MESH)
        pl.semaphore_wait(barrier, 5 + cols - 1)

    @pl.when(is_end)
    def _():
        pl.semaphore_wait(barrier, 4 + cols - 1)

    def remote(source, target, send_sem, recv_sem, device):
        return pltpu.make_async_remote_copy(
            src_ref=source, dst_ref=target, send_sem=send_sem, recv_sem=recv_sem,
            device_id=device, device_id_type=MESH,
        )

    def t_rows(level, m, k, col, children=None):
        here = pl.ds(col * rows, rows)
        if children is None:
            source, target = t_in.at[level, m], t.at[level, m, :, here, :]
        else:
            source, target = t_in.at[level, m, children], t.at[level, m, children, here, :]
        group = 0 if level < 2 else 1 if children is None else 2
        return remote(
            source, target, t_send.at[group, k - 1], t_recv.at[level, m, k - 1], {"col": (my_col + k) % cols}
        )

    def wait_rows(level, m, children=None):
        for k in range(1, cols):
            t_rows(level, m, k, (my_col + cols - k) % cols, children).wait_recv()

    own_side = pl.ds(side, 2)

    order = sorted(
        (2 * m + (0, 1, 3)[level], level, m) for m in range(nodes_here) for level in range(3) if (level, m) != (2, last)
    )
    for _, level, m in order:
        for k in range(1, cols):
            t_rows(level, m, k, my_col).start()

    def t_sum_copy(who, device):
        return remote(
            t_in.at[2, last, pl.ds(other, 2)], t_sum.at[who, :, my_rows, :],
            sum_send.at[0], sum_recv.at[who], {"node": device},
        )

    @pl.when(is_mid)
    def _():
        t_sum_copy(0, by_across).start()

    @pl.when(is_end)
    def _():
        t_sum_copy(1, by_cross).start()

    def spread(k, col):
        part = t_sum.at[:, :, pl.ds(col * rows, rows), :]
        return remote(part, part, spread_send.at[k - 1], spread_recv.at[k - 1], {"col": (my_col + k) % cols})

    def copy(kind, u):
        source, target, device = {
            TO_TWO: lambda: (held.at[u, 0], held.at[u, 1], by_two),
            FORWARD: lambda: (held.at[u], theirs.at[u], by_core),
            TO_PAIR: lambda: (y1.at[u], pair.at[u], by_pair),
            TO_ACROSS: lambda: (y1.at[u], across.at[u], by_across),
            RELAY: lambda: (pair.at[u], relayed.at[u], by_across),
            PARTIAL: lambda: (partial_out.at[u], partial_in.at[u], by_pair),
            SUM_NEAR: lambda: (sums.at[0, u - plain], across.at[u], by_across),
            SUM_FAR: lambda: (sums.at[1, u - plain], partial_in.at[u], by_cross),
        }[kind]()
        return remote(source, target, send.at[kind], recv.at[ROW[kind], u], {"node": device})

    def sent(kind, source, target):
        remote(source, target, send.at[kind], recv.at[ROW[kind], 0], {"node": by_pair}).wait_send()

    def far(m):
        return remote(
            t.at[2, m, pl.ds(1 - two // 3, 3)], t_far.at[m], far_send.at[0], far_recv.at[m], {"node": by_pair}
        )

    def store(u, total):
        columns = pl.ds(pl.multiple_of(u % chunks * width, width), width)
        out_ref[u // chunks, :, columns] = total.astype(out_ref.dtype)

    def first(u, action):
        @pl.when(u % chunks == 0)
        def _():
            action(u // chunks)

    def stage_zero(u):
        first(u, lambda m: wait_rows(0, m))
        m = u // chunks
        columns = pl.ds(pl.multiple_of(u % chunks * width, width), width)
        total = dot(t[0, m, 0], x[0, :, columns])
        for j in range(1, 4):
            total += dot(t[0, m, j], x[j, :, columns])
        held[u, 0] = total.astype(held.dtype)
        copy(TO_TWO, u).start()

    def stage_one(u):
        copy(TO_TWO, u).wait_recv()
        copy(FORWARD, u).start()
        first(u, lambda m: wait_rows(1, m))
        m = u // chunks
        total = dot(t[1, m, one], held[u, 0])
        total += dot(t[1, m, flip(one, 2)], held[u, 1])
        copy(FORWARD, u).wait_recv()
        total += dot(t[1, m, flip(one, 1)], theirs[u, 0])
        total += dot(t[1, m, 3 - one], theirs[u, 1])
        y1[u] = total.astype(y1.dtype)

        @pl.when(is_mid & (u < plain))
        def _():
            copy(TO_ACROSS, u).start()

        @pl.when(is_end | (u >= plain))
        def _():
            copy(TO_PAIR, u).start()

    def stage_relay(u):
        copy(TO_PAIR, u).wait_recv()

        @pl.when(u < plain)
        def _():
            copy(RELAY, u).start()

        @pl.when(u >= plain)
        def _():
            @pl.when(u == plain)
            def _():
                for k in range(1, cols):
                    spread(k, (my_col + cols - k) % cols).wait_recv()

            for who, kind in ((1, SUM_FAR), (0, SUM_NEAR)):
                total = dot(t_sum[who, two % 2], y1[u]) + dot(t_sum[who, 1 - two % 2], pair[u])
                sums[who, u - plain] = total.astype(sums.dtype)
                copy(kind, u).start()

    def stage_far(u):
        def send_far(m):
            wait_rows(2, m)
            far(m).start()

        @pl.when(u < plain)
        def _():
            first(u, send_far)

    def own_part(u):
        m = u // chunks
        return dot(t[2, m, two], y1[u])

    def pair_part(u):
        return dot(t[2, u // chunks, flip(two, 1)], pair[u])

    def stage_mid(u):
        @pl.when(u < plain)
        def _():
            def arrive(m):
                wait_rows(2, m)
                far(m).wait_recv()

            first(u, arrive)
            m = u // chunks
            copy(TO_ACROSS, u).wait_recv()
            copy(RELAY, u).wait_recv()
            start = 1 - two // 2
            part = dot(t_far[m, 3 - two - start], across[u])
            part += dot(t_far[m, flip(3 - two, 1) - start], relayed[u])
            part += dot(t_far[m, two - start], y1[u])
            partial_out[u] = part.astype(partial_out.dtype)
            copy(PARTIAL, u).start()
            total = own_part(u) + pair_part(u)
            total += dot(t[2, m, 3 - two], across[u])
            total += dot(t[2, m, flip(two, 2)], relayed[u])
            store(u, total)

        @pl.when(u >= plain)
        def _():
            @pl.when(u == plain)
            def _():
                wait_rows(2, last, own_side)

            total = own_part(u) + pair_part(u)
            copy(SUM_NEAR, u).wait_recv()
            store(u, total + across[u].astype(jnp.float32))

    def stage_end(u):
        @pl.when(u < plain)
        def _():
            total = own_part(u)
            copy(PARTIAL, u).wait_recv()
            store(u, total + partial_in[u].astype(jnp.float32))

        @pl.when(u >= plain)
        def _():
            @pl.when(u == plain)
            def _():
                wait_rows(2, last, own_side)

            copy(TO_PAIR, u).wait_recv()
            total = own_part(u) + pair_part(u)
            copy(SUM_FAR, u).wait_recv()
            store(u, total + partial_in[u].astype(jnp.float32))

    x_copy.wait()
    t_copy.wait()

    def step(s, _):
        def run(stage, lag, role=None):
            u = s - lag
            ready = (u >= 0) & (u < units)

            @pl.when(ready if role is None else ready & role)
            def _():
                stage(u)

        run(stage_one, LAG_ONE)

        @pl.when(s == LAG_ONE)
        def _():
            @pl.when(is_mid)
            def _():
                for who, device in enumerate((by_across, by_cross)):
                    t_sum_copy(who, device).wait_recv()
                for k in range(1, cols):
                    spread(k, my_col).start()

            for k in range(1, cols):
                t_rows(2, last, k, my_col, own_side).start()

        run(stage_relay, LAG_RELAY, is_mid)
        run(stage_far, LAG_FAR, is_end)
        run(stage_mid, LAG_MID, is_mid)
        run(stage_end, LAG_END, is_end)
        run(stage_zero, 0)
        return 0

    lax.fori_loop(0, units + LAG_END, step, 0)

    sent(TO_TWO, held.at[:, 0], held.at[:, 1])
    sent(FORWARD, held, theirs)

    @pl.when(is_mid)
    def _():
        early = pl.ds(0, plain)
        late = pl.ds(plain, units - plain)
        sent(TO_PAIR, y1.at[late], pair.at[late])
        sent(TO_ACROSS, y1.at[early], across.at[early])
        sent(RELAY, pair.at[early], relayed)
        sent(PARTIAL, partial_out, partial_in.at[early])
        sent(SUM_NEAR, sums.at[0], across.at[late])
        sent(SUM_FAR, sums.at[1], across.at[late])
        for k in range(1, cols):
            spread(k, my_col).wait_send()

    @pl.when(is_end)
    def _():
        sent(TO_PAIR, y1, pair)
        remote(t_far, t_far, far_send.at[0], far_recv.at[0], {"node": by_pair}).wait_send()

    t_sum_copy(0, by_across).wait_send()
    for k in range(1, cols):
        beside = {"col": (my_col + k) % cols}
        both, rest = t_in.at[pl.ds(0, 2)], t_in.at[2, pl.ds(0, last)]
        remote(both, t.at[pl.ds(0, 2), :, :, my_rows, :], t_send.at[0, k - 1], t_recv.at[0, 0, k - 1], beside).wait_send()
        remote(
            rest, t.at[2, pl.ds(0, last), :, my_rows, :], t_send.at[1, k - 1], t_recv.at[0, 0, k - 1], beside
        ).wait_send()
        t_rows(2, last, k, my_col, own_side).wait_send()


def local(coefficients, transfer):
    cols = lax.axis_size("col")
    nodes_here, rank, columns = coefficients.shape
    levels, _, children, rows, _ = transfer.shape
    width = min(WIDTH, columns)
    chunks = columns // width
    units = nodes_here * chunks
    plain = units - chunks
    others = max(cols - 1, 1)
    kind = coefficients.dtype
    block = (rank, width)
    dma = pltpu.SemaphoreType.DMA
    return pl.pallas_call(
        functools.partial(kernel, cols, chunks),
        out_shape=pltpu.VMEM(coefficients.shape, kind),
        in_specs=[pl.BlockSpec(memory_space=pl.ANY)] * 2,
        out_specs=pl.BlockSpec(memory_space=pltpu.VMEM),
        scratch_shapes=[
            pltpu.VMEM(coefficients.shape, kind),
            pltpu.VMEM((levels, nodes_here, children, rank, rank), kind),
            pltpu.VMEM((nodes_here - 1, children - 1, rank, rank), kind),
            pltpu.VMEM((2, 2, rank, rank), kind),
            pltpu.VMEM((units, 2) + block, kind),
            pltpu.VMEM((units, 2) + block, kind),
            pltpu.VMEM((units,) + block, kind),
            pltpu.VMEM((units,) + block, kind),
            pltpu.VMEM((units,) + block, kind),
            pltpu.VMEM((plain,) + block, kind),
            pltpu.VMEM((plain,) + block, kind),
            pltpu.VMEM((units,) + block, kind),
            pltpu.VMEM((2, chunks) + block, kind),
            dma((2,)),
            dma((8,)),
            dma((5, units)),
            dma((3, others)),
            dma((levels, nodes_here, others)),
            dma((1,)),
            dma((nodes_here - 1,)),
            dma((1,)),
            dma((2,)),
            dma((others,)),
            dma((others,)),
        ],
        compiler_params=pltpu.CompilerParams(
            collective_id=0, has_side_effects=True, vmem_limit_bytes=56 * 1024 * 1024
        ),
    )(coefficients, transfer)


def solution(mesh):
    return jax.shard_map(
        local,
        mesh=mesh,
        in_specs=(P("node", None, "col"), P(None, "node", None, "col", None)),
        out_specs=P("node", None, "col"),
        check_vma=False,
    )
```

time: 125 us -> 118 us (0.944)
  Pallas kernels: 122 us -> 117 us
  local copies, waits for them, and re-layouts: 3.08 us -> 1.32 us
    pallas_call x1, Pallas kernels: 122 us -> 117 us  [local(): pl.pallas_call(functools.partial(kernel, cols, chunks), out_shape=pltpu.V...]
    unnamed x1, local copies, waits for them, and re-layouts: 3.08 us -> 1.32 us
where the time goes in v1:
time: 118 us
  Pallas kernels  117 us (99%)
  local copies, waits for them, and re-layouts  1.32 us (1%)
    pallas_call x1, Pallas kernels, local(): pl.pallas_call(functools.partial(kernel, cols, chunks), out_shape=pltpu.V...  117 us

profile of v1, /device:TPU:0, one launch (start us, length us, event | category | flops | bytes accessed | tf_op | source)
XLA Modules:
  0.0 118.3 jit_solution(9564541167869579686)
XLA Ops:
  0.0 117.0 %shard_map.28 = bf16[4,256,1024]{2,1,0:T(8,128)(2,1)S(1)} custom-call(bf16[4,256,1024]{2,1,0:T(8,128)(2,1)} %x_in.1, bf16[3,4,4,128,256]{4,3,2,1,0:T(8,128)(2,1)} %t_in.1), custom_call_target="tpu_custom_call" | custom-call | tf_op jit(solution)/shard_map/pallas_call | solution.py:340
  117.0 1.3 %copy.4 = bf16[4,256,1024]{2,1,0:T(8,128)(2,1)} copy(bf16[4,256,1024]{2,1,0:T(8,128)(2,1)S(1)} %shard_map.28) | data formatting | bytes 4194304

commit v2 on v1

--- a/solution.py
+++ b/solution.py
@@ -9,9 +9,10 @@
 
 MESH = pl.DeviceIdType.MESH
 WIDTH = 256
-LAG_ONE, LAG_RELAY, LAG_FAR, LAG_MID, LAG_END = 3, 5, 8, 11, 13
+HELD_BACK = 2
+LAG_ONE, LAG_RELAY, LAG_FAR, LAG_MID, LAG_NEAR, LAG_END = 2, 4, 5, 7, 8, 10
 TO_TWO, FORWARD, TO_PAIR, TO_ACROSS, RELAY, PARTIAL, SUM_NEAR, SUM_FAR = range(8)
-ROW = {TO_TWO: 0, FORWARD: 1, TO_PAIR: 2, TO_ACROSS: 3, RELAY: 4, PARTIAL: 3, SUM_NEAR: 3, SUM_FAR: 3}
+ROW = {TO_TWO: 0, FORWARD: 1, TO_PAIR: 2, TO_ACROSS: 3, RELAY: 4, PARTIAL: 3, SUM_NEAR: 3, SUM_FAR: 4}
 
 
 def flip(i, bit):
@@ -24,7 +25,7 @@
 
 def kernel(
     cols, chunks, x_in, t_in, out_ref,
-    x, t, t_far, t_sum, held, theirs, y1, pair, across, relayed, partial_out, partial_in, sums,
+    x, t, t_far, t_pass, t_sum, held, theirs, y1, pair, across, relayed, partial_out, partial_in, sums,
     local_sem, send, recv, t_send, t_recv, far_send, far_recv, sum_send, sum_recv, spread_send, spread_recv,
 ):
     nodes_here = x_in.shape[0]
@@ -41,7 +42,7 @@
     other = 2 - side
     is_mid = (two + 1) // 2 % 2 == 1
     is_end = (two + 1) // 2 % 2 == 0
-    by_core, by_two, by_pair, by_cross = flip(me, 1), flip(me, 2), flip(me, 4), flip(me, 8)
+    by_core, by_two, by_pair = flip(me, 1), flip(me, 2), flip(me, 4)
     by_across = flip(by_pair, 8)
     my_rows = pl.ds(my_col * rows, rows)
 
@@ -53,17 +54,17 @@
     barrier = pltpu.get_barrier_semaphore()
     for k in range(1, cols):
         pl.semaphore_signal(barrier, inc=1, device_id={"col": (my_col + k) % cols}, device_id_type=MESH)
-    for device in (by_cross, by_pair, by_two, by_core):
+    for device in (by_pair, by_two, by_core):
         pl.semaphore_signal(barrier, inc=1, device_id={"node": device}, device_id_type=MESH)
 
     @pl.when(is_mid)
     def _():
         pl.semaphore_signal(barrier, inc=1, device_id={"node": by_across}, device_id_type=MESH)
-        pl.semaphore_wait(barrier, 5 + cols - 1)
+        pl.semaphore_wait(barrier, 4 + cols - 1)
 
     @pl.when(is_end)
     def _():
-        pl.semaphore_wait(barrier, 4 + cols - 1)
+        pl.semaphore_wait(barrier, 3 + cols - 1)
 
     def remote(source, target, send_sem, recv_sem, device):
         return pltpu.make_async_remote_copy(
@@ -89,25 +90,30 @@
     own_side = pl.ds(side, 2)
 
     order = sorted(
-        (2 * m + (0, 1, 3)[level], level, m) for m in range(nodes_here) for level in range(3) if (level, m) != (2, last)
+        (3 * m + 2 * level, level, m) for m in range(nodes_here) for level in range(3) if (level, m) != (2, last)
     )
     for _, level, m in order:
         for k in range(1, cols):
             t_rows(level, m, k, my_col).start()
 
-    def t_sum_copy(who, device):
-        return remote(
-            t_in.at[2, last, pl.ds(other, 2)], t_sum.at[who, :, my_rows, :],
-            sum_send.at[0], sum_recv.at[who], {"node": device},
-        )
+    given = t_in.at[2, last, pl.ds(other, 2)]
+
+    def give():
+        return remote(given, t_sum.at[0, :, my_rows, :], sum_send.at[0], sum_recv.at[0], {"node": by_across})
+
+    def give_pair():
+        return remote(given, t_pass, sum_send.at[0], sum_recv.at[2], {"node": by_pair})
+
+    def give_on():
+        return remote(t_pass, t_sum.at[1, :, my_rows, :], sum_send.at[1], sum_recv.at[1], {"node": by_across})
 
     @pl.when(is_mid)
     def _():
-        t_sum_copy(0, by_across).start()
+        give().start()
 
     @pl.when(is_end)
     def _():
-        t_sum_copy(1, by_cross).start()
+        give_pair().start()
 
     def spread(k, col):
         part = t_sum.at[:, :, pl.ds(col * rows, rows), :]
@@ -122,7 +128,7 @@
             RELAY: lambda: (pair.at[u], relayed.at[u], by_across),
             PARTIAL: lambda: (partial_out.at[u], partial_in.at[u], by_pair),
             SUM_NEAR: lambda: (sums.at[0, u - plain], across.at[u], by_across),
-            SUM_FAR: lambda: (sums.at[1, u - plain], partial_in.at[u], by_cross),
+            SUM_FAR: lambda: (sums.at[1, u - plain], relayed.at[u], by_across),
         }[kind]()
         return remote(source, target, send.at[kind], recv.at[ROW[kind], u], {"node": device})
 
@@ -130,9 +136,11 @@
         remote(source, target, send.at[kind], recv.at[ROW[kind], 0], {"node": by_pair}).wait_send()
 
     def far(m):
-        return remote(
-            t.at[2, m, pl.ds(1 - two // 3, 3)], t_far.at[m], far_send.at[0], far_recv.at[m], {"node": by_pair}
-        )
+        if isinstance(m, int) and m == last:
+            source, target, sem = t.at[2, m, flip(two, 1)], t_far.at[m, 0], far_send.at[1]
+        else:
+            source, target, sem = t.at[2, m, pl.ds(1 - two // 3, 3)], t_far.at[m], far_send.at[0]
+        return remote(source, target, sem, far_recv.at[m], {"node": by_pair})
 
     def store(u, total):
         columns = pl.ds(pl.multiple_of(u % chunks * width, width), width)
@@ -143,15 +151,37 @@
         def _():
             action(u // chunks)
 
+    def zero_rows(u, here):
+        columns = pl.ds(pl.multiple_of(u % chunks * width, width), width)
+        total = dot(t[0, 0, 0, here], x[0, :, columns])
+        for j in range(1, 4):
+            total += dot(t[0, 0, j, here], x[j, :, columns])
+        held[u, 0, here] = total.astype(held.dtype)
+        remote(
+            held.at[u, 0, here], held.at[u, 1, here], send.at[TO_TWO], recv.at[ROW[TO_TWO], u], {"node": by_two}
+        ).start()
+
+    def own_rows(u, _):
+        zero_rows(u, pl.ds(pl.multiple_of(my_col * rows, rows), rows))
+        return 0
+
     def stage_zero(u):
         first(u, lambda m: wait_rows(0, m))
-        m = u // chunks
-        columns = pl.ds(pl.multiple_of(u % chunks * width, width), width)
-        total = dot(t[0, m, 0], x[0, :, columns])
-        for j in range(1, 4):
-            total += dot(t[0, m, j], x[j, :, columns])
-        held[u, 0] = total.astype(held.dtype)
-        copy(TO_TWO, u).start()
+
+        @pl.when(u < chunks)
+        def _():
+            for k in range(1, cols):
+                zero_rows(u, pl.ds(pl.multiple_of((my_col + k) % cols * rows, rows), rows))
+
+        @pl.when(u >= chunks)
+        def _():
+            m = u // chunks
+            columns = pl.ds(pl.multiple_of(u % chunks * width, width), width)
+            total = dot(t[0, m, 0], x[0, :, columns])
+            for j in range(1, 4):
+                total += dot(t[0, m, j], x[j, :, columns])
+            held[u, 0] = total.astype(held.dtype)
+            copy(TO_TWO, u).start()
 
     def stage_one(u):
         copy(TO_TWO, u).wait_recv()
@@ -169,7 +199,7 @@
         def _():
             copy(TO_ACROSS, u).start()
 
-        @pl.when(is_end | (u >= plain))
+        @pl.when(is_end)
         def _():
             copy(TO_PAIR, u).start()
 
@@ -190,16 +220,21 @@
             for who, kind in ((1, SUM_FAR), (0, SUM_NEAR)):
                 total = dot(t_sum[who, two % 2], y1[u]) + dot(t_sum[who, 1 - two % 2], pair[u])
                 sums[who, u - plain] = total.astype(sums.dtype)
-                copy(kind, u).start()
-
-    def stage_far(u):
-        def send_far(m):
-            wait_rows(2, m)
-            far(m).start()
-
-        @pl.when(u < plain)
-        def _():
-            first(u, send_far)
+                if kind == SUM_FAR:
+                    copy(kind, u).start()
+
+            @pl.when(u < units - HELD_BACK)
+            def _():
+                copy(SUM_NEAR, u).start()
+
+            @pl.when(u == units - 1)
+            def _():
+                for late in range(min(HELD_BACK, chunks), 0, -1):
+                    copy(SUM_NEAR, units - late).start()
+
+    def stage_far(m):
+        wait_rows(2, m, own_side if m == last else None)
+        far(m).start()
 
     def own_part(u):
         m = u // chunks
@@ -235,31 +270,33 @@
             @pl.when(u == plain)
             def _():
                 wait_rows(2, last, own_side)
-
+                far(last).wait_recv()
+
+            copy(SUM_FAR, u).wait_recv()
+            part = dot(t_far[last, 0], y1[u]) + relayed[u].astype(jnp.float32)
+            partial_out[u] = part.astype(partial_out.dtype)
+            copy(PARTIAL, u).start()
+
+    def stage_near(u):
+        @pl.when(u >= plain)
+        def _():
             total = own_part(u) + pair_part(u)
             copy(SUM_NEAR, u).wait_recv()
             store(u, total + across[u].astype(jnp.float32))
 
     def stage_end(u):
-        @pl.when(u < plain)
-        def _():
-            total = own_part(u)
-            copy(PARTIAL, u).wait_recv()
-            store(u, total + partial_in[u].astype(jnp.float32))
-
-        @pl.when(u >= plain)
-        def _():
-            @pl.when(u == plain)
-            def _():
-                wait_rows(2, last, own_side)
-
-            copy(TO_PAIR, u).wait_recv()
-            total = own_part(u) + pair_part(u)
-            copy(SUM_FAR, u).wait_recv()
-            store(u, total + partial_in[u].astype(jnp.float32))
+        total = own_part(u)
+        copy(PARTIAL, u).wait_recv()
+        store(u, total + partial_in[u].astype(jnp.float32))
 
     x_copy.wait()
     t_copy.wait()
+    lax.fori_loop(0, chunks, own_rows, 0)
+
+    @pl.when(is_mid)
+    def _():
+        give_pair().wait_recv()
+        give_on().start()
 
     def step(s, _):
         def run(stage, lag, role=None):
@@ -270,25 +307,31 @@
             def _():
                 stage(u)
 
+        run(stage_relay, LAG_RELAY, is_mid)
         run(stage_one, LAG_ONE)
 
         @pl.when(s == LAG_ONE)
         def _():
             @pl.when(is_mid)
             def _():
-                for who, device in enumerate((by_across, by_cross)):
-                    t_sum_copy(who, device).wait_recv()
+                give().wait_recv()
+                give_on().wait_recv()
                 for k in range(1, cols):
                     spread(k, my_col).start()
 
             for k in range(1, cols):
                 t_rows(2, last, k, my_col, own_side).start()
 
-        run(stage_relay, LAG_RELAY, is_mid)
-        run(stage_far, LAG_FAR, is_end)
+        run(stage_zero, 0)
+        for m in range(nodes_here):
+
+            @pl.when(is_end & (s == LAG_FAR + m * chunks))
+            def _(m=m):
+                stage_far(m)
+
         run(stage_mid, LAG_MID, is_mid)
+        run(stage_near, LAG_NEAR, is_mid)
         run(stage_end, LAG_END, is_end)
-        run(stage_zero, 0)
         return 0
 
     lax.fori_loop(0, units + LAG_END, step, 0)
@@ -300,21 +343,24 @@
     def _():
         early = pl.ds(0, plain)
         late = pl.ds(plain, units - plain)
-        sent(TO_PAIR, y1.at[late], pair.at[late])
         sent(TO_ACROSS, y1.at[early], across.at[early])
-        sent(RELAY, pair.at[early], relayed)
-        sent(PARTIAL, partial_out, partial_in.at[early])
+        sent(RELAY, pair.at[early], relayed.at[early])
+        sent(PARTIAL, partial_out, partial_in)
         sent(SUM_NEAR, sums.at[0], across.at[late])
         sent(SUM_FAR, sums.at[1], across.at[late])
+        give().wait_send()
+        give_on().wait_send()
         for k in range(1, cols):
             spread(k, my_col).wait_send()
 
     @pl.when(is_end)
     def _():
         sent(TO_PAIR, y1, pair)
-        remote(t_far, t_far, far_send.at[0], far_recv.at[0], {"node": by_pair}).wait_send()
-
-    t_sum_copy(0, by_across).wait_send()
+        whole = t_far.at[pl.ds(0, last)]
+        remote(whole, whole, far_send.at[0], far_recv.at[0], {"node": by_pair}).wait_send()
+        far(last).wait_send()
+        give_pair().wait_send()
+
     for k in range(1, cols):
         beside = {"col": (my_col + k) % cols}
         both, rest = t_in.at[pl.ds(0, 2)], t_in.at[2, pl.ds(0, last)]
@@ -345,15 +391,16 @@
         scratch_shapes=[
             pltpu.VMEM(coefficients.shape, kind),
             pltpu.VMEM((levels, nodes_here, children, rank, rank), kind),
-            pltpu.VMEM((nodes_here - 1, children - 1, rank, rank), kind),
+            pltpu.VMEM((nodes_here, children - 1, rank, rank), kind),
+            pltpu.VMEM((2, rows, rank), kind),
             pltpu.VMEM((2, 2, rank, rank), kind),
             pltpu.VMEM((units, 2) + block, kind),
             pltpu.VMEM((units, 2) + block, kind),
             pltpu.VMEM((units,) + block, kind),
             pltpu.VMEM((units,) + block, kind),
             pltpu.VMEM((units,) + block, kind),
-            pltpu.VMEM((plain,) + block, kind),
-            pltpu.VMEM((plain,) + block, kind),
+            pltpu.VMEM((units,) + block, kind),
+            pltpu.VMEM((units,) + block, kind),
             pltpu.VMEM((units,) + block, kind),
             pltpu.VMEM((2, chunks) + block, kind),
             dma((2,)),
@@ -361,10 +408,10 @@
             dma((5, units)),
             dma((3, others)),
             dma((levels, nodes_here, others)),
-            dma((1,)),
-            dma((nodes_here - 1,)),
-            dma((1,)),
             dma((2,)),
+            dma((nodes_here,)),
+            dma((2,)),
+            dma((3,)),
             dma((others,)),
             dma((others,)),
         ],

time: 118 us -> 112 us (0.949)
  the two profiles are of different devices: /device:TPU:0 before, /device:TPU:8 now
where the time goes in v2:
time: 112 us; the launch traced here: 111 us
  Pallas kernels  110 us (98%)
  local copies, waits for them, and re-layouts  1.32 us (1%)
    pallas_call x1, Pallas kernels, local(): pl.pallas_call(functools.partial(kernel, cols, chunks), out_shape=pltpu.V...  110 us

profile of v2, /device:TPU:8, one launch (start us, length us, event | category | flops | bytes accessed | tf_op | source)
XLA Modules:
  0.0 111.2 jit_solution(8071800367910022000)
XLA Ops:
  0.0 109.9 %shard_map.28 = bf16[4,256,1024]{2,1,0:T(8,128)(2,1)S(1)} custom-call(bf16[4,256,1024]{2,1,0:T(8,128)(2,1)} %x_in.1, bf16[3,4,4,128,256]{4,3,2,1,0:T(8,128)(2,1)} %t_in.1), custom_call_target="tpu_custom_call" | custom-call | tf_op jit(solution)/shard_map/pallas_call | solution.py:386
  109.9 1.3 %copy.4 = bf16[4,256,1024]{2,1,0:T(8,128)(2,1)} copy(bf16[4,256,1024]{2,1,0:T(8,128)(2,1)S(1)} %shard_map.28) | data formatting | bytes 4194304

commit v3 on v2

--- a/solution.py
+++ b/solution.py
@@ -9,8 +9,8 @@
 
 MESH = pl.DeviceIdType.MESH
 WIDTH = 256
-HELD_BACK = 2
-LAG_ONE, LAG_RELAY, LAG_FAR, LAG_MID, LAG_NEAR, LAG_END = 2, 4, 5, 7, 8, 10
+HELD_BACK = 3
+LAG_ONE, LAG_RELAY, LAG_FAR, LAG_MID, LAG_NEAR, LAG_END = 2, 5, 4, 9, 13, 12
 TO_TWO, FORWARD, TO_PAIR, TO_ACROSS, RELAY, PARTIAL, SUM_NEAR, SUM_FAR = range(8)
 ROW = {TO_TWO: 0, FORWARD: 1, TO_PAIR: 2, TO_ACROSS: 3, RELAY: 4, PARTIAL: 3, SUM_NEAR: 3, SUM_FAR: 4}
 
@@ -307,9 +307,10 @@
             def _():
                 stage(u)
 
+        run(stage_mid, LAG_MID, is_mid)
+        run(stage_near, LAG_NEAR, is_mid)
         run(stage_relay, LAG_RELAY, is_mid)
         run(stage_one, LAG_ONE)
-
         @pl.when(s == LAG_ONE)
         def _():
             @pl.when(is_mid)
@@ -329,12 +330,10 @@
             def _(m=m):
                 stage_far(m)
 
-        run(stage_mid, LAG_MID, is_mid)
-        run(stage_near, LAG_NEAR, is_mid)
         run(stage_end, LAG_END, is_end)
         return 0
 
-    lax.fori_loop(0, units + LAG_END, step, 0)
+    lax.fori_loop(0, units + max(LAG_NEAR, LAG_END), step, 0)
 
     sent(TO_TWO, held.at[:, 0], held.at[:, 1])
     sent(FORWARD, held, theirs)

time: 112 us -> 111 us (level)
  no operation moved by 1% of the time
where the time goes in v3:
time: 111 us
  Pallas kernels  110 us (99%)
  local copies, waits for them, and re-layouts  1.32 us (1%)
    pallas_call x1, Pallas kernels, local(): pl.pallas_call(functools.partial(kernel, cols, chunks), out_shape=pltpu.V...  110 us

profile of v3, /device:TPU:8, one launch (start us, length us, event | category | flops | bytes accessed | tf_op | source)
XLA Modules:
  0.0 111.2 jit_solution(8822462453660143896)
XLA Ops:
  0.0 109.9 %shard_map.28 = bf16[4,256,1024]{2,1,0:T(8,128)(2,1)S(1)} custom-call(bf16[4,256,1024]{2,1,0:T(8,128)(2,1)} %x_in.1, bf16[3,4,4,128,256]{4,3,2,1,0:T(8,128)(2,1)} %t_in.1), custom_call_target="tpu_custom_call" | custom-call | tf_op jit(solution)/shard_map/pallas_call | solution.py:385
  109.9 1.3 %copy.4 = bf16[4,256,1024]{2,1,0:T(8,128)(2,1)} copy(bf16[4,256,1024]{2,1,0:T(8,128)(2,1)S(1)} %shard_map.28) | data formatting | bytes 4194304

commit v4 on v3

--- a/solution.py
+++ b/solution.py
@@ -9,8 +9,8 @@
 
 MESH = pl.DeviceIdType.MESH
 WIDTH = 256
-HELD_BACK = 3
-LAG_ONE, LAG_RELAY, LAG_FAR, LAG_MID, LAG_NEAR, LAG_END = 2, 5, 4, 9, 13, 12
+HELD_BACK = 4
+LAG_ONE, LAG_RELAY, LAG_FAR, LAG_MID, LAG_NEAR, LAG_END = 2, 4, 5, 8, 12, 10
 TO_TWO, FORWARD, TO_PAIR, TO_ACROSS, RELAY, PARTIAL, SUM_NEAR, SUM_FAR = range(8)
 ROW = {TO_TWO: 0, FORWARD: 1, TO_PAIR: 2, TO_ACROSS: 3, RELAY: 4, PARTIAL: 3, SUM_NEAR: 3, SUM_FAR: 4}
 
@@ -26,7 +26,7 @@
 def kernel(
     cols, chunks, x_in, t_in, out_ref,
     x, t, t_far, t_pass, t_sum, held, theirs, y1, pair, across, relayed, partial_out, partial_in, sums,
-    local_sem, send, recv, t_send, t_recv, far_send, far_recv, sum_send, sum_recv, spread_send, spread_recv,
+    local_sem, send, recv, half_x, half_core, t_send, t_recv, far_send, far_recv, sum_send, sum_recv, spread_send, spread_recv,
 ):
     nodes_here = x_in.shape[0]
     last = nodes_here - 1
@@ -151,37 +151,82 @@
         def _():
             action(u // chunks)
 
-    def zero_rows(u, here):
-        columns = pl.ds(pl.multiple_of(u % chunks * width, width), width)
-        total = dot(t[0, 0, 0, here], x[0, :, columns])
+    def all_columns(u):
+        return pl.ds(pl.multiple_of(u % chunks * width, width), width)
+
+    def piece_to_two(u, here, columns, sem):
+        return remote(held.at[u, 0, here, columns], held.at[u, 1, here, columns], send.at[TO_TWO], sem, {"node": by_two})
+
+    def zero_rows(u, here, wanted, columns, sem):
+        total = dot(t[0, 0, 0, here], x[0, :, wanted])
         for j in range(1, 4):
-            total += dot(t[0, 0, j, here], x[j, :, columns])
-        held[u, 0, here] = total.astype(held.dtype)
-        remote(
-            held.at[u, 0, here], held.at[u, 1, here], send.at[TO_TWO], recv.at[ROW[TO_TWO], u], {"node": by_two}
-        ).start()
+            total += dot(t[0, 0, j, here], x[j, :, wanted])
+        held[u, 0, here, columns] = total.astype(held.dtype)
+        piece_to_two(u, here, columns, sem).start()
+
+    def rows_of(k):
+        return pl.ds(pl.multiple_of((my_col + k) % cols * rows, rows), rows)
+
+    whole = pl.ds(0, width)
 
     def own_rows(u, _):
-        zero_rows(u, pl.ds(pl.multiple_of(my_col * rows, rows), rows))
+        zero_rows(u, rows_of(0), all_columns(u), whole, recv.at[ROW[TO_TWO], u])
         return 0
+
+    def other_rows(u, _):
+        for k in range(1, cols):
+            zero_rows(u, rows_of(k), all_columns(u), whole, recv.at[ROW[TO_TWO], u])
+        return 0
+
+    halves = [pl.ds(h * width // 2, width // 2) for h in range(2)]
+
+    def half_to_core(h):
+        source, target = held.at[0, :, :, halves[h]], theirs.at[0, :, :, halves[h]]
+        return remote(source, target, send.at[FORWARD], half_core.at[h], {"node": by_core})
+
+    def one_rows(here, columns):
+        total = dot(t[1, 0, one, here], held[0, 0, :, columns])
+        total += dot(t[1, 0, flip(one, 2), here], held[0, 1, :, columns])
+        total += dot(t[1, 0, flip(one, 1), here], theirs[0, 0, :, columns])
+        total += dot(t[1, 0, 3 - one, here], theirs[0, 1, :, columns])
+        y1[0, here, columns] = total.astype(y1.dtype)
+
+        def part(kind, target, device):
+            remote(
+                y1.at[0, here, columns], target.at[0, here, columns],
+                send.at[kind], recv.at[ROW[kind], 0], {"node": device},
+            ).start()
+
+        pl.when(is_mid)(lambda: part(TO_ACROSS, across, by_across))
+        pl.when(is_end)(lambda: part(TO_PAIR, pair, by_pair))
+
+    def first_unit():
+        wait_rows(0, 0)
+        for h in range(2):
+            for k in range(1, cols):
+                zero_rows(0, rows_of(k), halves[h], halves[h], half_x.at[h, k - 1])
+        lax.fori_loop(1, chunks, other_rows, 0)
+        piece_to_two(0, rows_of(0), whole, recv.at[ROW[TO_TWO], 0]).wait_recv()
+        for h in range(2):
+            for k in range(1, cols):
+                piece_to_two(0, rows_of(k), halves[h], half_x.at[h, k - 1]).wait_recv()
+            half_to_core(h).start()
+        for h in range(2):
+            half_to_core(h).wait_recv()
+            one_rows(rows_of(0), halves[h])
+        wait_rows(1, 0)
+        for k in range(1, cols):
+            one_rows(rows_of(k), whole)
 
     def stage_zero(u):
         first(u, lambda m: wait_rows(0, m))
-
-        @pl.when(u < chunks)
-        def _():
-            for k in range(1, cols):
-                zero_rows(u, pl.ds(pl.multiple_of((my_col + k) % cols * rows, rows), rows))
-
-        @pl.when(u >= chunks)
-        def _():
-            m = u // chunks
-            columns = pl.ds(pl.multiple_of(u % chunks * width, width), width)
-            total = dot(t[0, m, 0], x[0, :, columns])
-            for j in range(1, 4):
-                total += dot(t[0, m, j], x[j, :, columns])
-            held[u, 0] = total.astype(held.dtype)
-            copy(TO_TWO, u).start()
+        m = u // chunks
+        columns = all_columns(u)
+        total = dot(t[0, m, 0], x[0, :, columns])
+        for j in range(1, 4):
+            total += dot(t[0, m, j], x[j, :, columns])
+        held[u, 0] = total.astype(held.dtype)
+        copy(TO_TWO, u).start()
 
     def stage_one(u):
         copy(TO_TWO, u).wait_recv()
@@ -298,10 +343,12 @@
         give_pair().wait_recv()
         give_on().start()
 
+    first_unit()
+
     def step(s, _):
-        def run(stage, lag, role=None):
+        def run(stage, lag, role=None, start=0):
             u = s - lag
-            ready = (u >= 0) & (u < units)
+            ready = (u >= start) & (u < units)
 
             @pl.when(ready if role is None else ready & role)
             def _():
@@ -310,8 +357,8 @@
         run(stage_mid, LAG_MID, is_mid)
         run(stage_near, LAG_NEAR, is_mid)
         run(stage_relay, LAG_RELAY, is_mid)
-        run(stage_one, LAG_ONE)
-        @pl.when(s == LAG_ONE)
+        run(stage_one, LAG_ONE, start=1)
+        @pl.when(s == LAG_ONE + 1)
         def _():
             @pl.when(is_mid)
             def _():
@@ -323,7 +370,7 @@
             for k in range(1, cols):
                 t_rows(2, last, k, my_col, own_side).start()
 
-        run(stage_zero, 0)
+        run(stage_zero, 0, start=chunks)
         for m in range(nodes_here):
 
             @pl.when(is_end & (s == LAG_FAR + m * chunks))
@@ -333,7 +380,7 @@
         run(stage_end, LAG_END, is_end)
         return 0
 
-    lax.fori_loop(0, units + max(LAG_NEAR, LAG_END), step, 0)
+    lax.fori_loop(LAG_ONE + 1, units + max(LAG_NEAR, LAG_END), step, 0)
 
     sent(TO_TWO, held.at[:, 0], held.at[:, 1])
     sent(FORWARD, held, theirs)
@@ -355,8 +402,8 @@
     @pl.when(is_end)
     def _():
         sent(TO_PAIR, y1, pair)
-        whole = t_far.at[pl.ds(0, last)]
-        remote(whole, whole, far_send.at[0], far_recv.at[0], {"node": by_pair}).wait_send()
+        full = t_far.at[pl.ds(0, last)]
+        remote(full, full, far_send.at[0], far_recv.at[0], {"node": by_pair}).wait_send()
         far(last).wait_send()
         give_pair().wait_send()
 
@@ -405,6 +452,8 @@
             dma((2,)),
             dma((8,)),
             dma((5, units)),
+            dma((2, others)),
+            dma((2,)),
             dma((3, others)),
             dma((levels, nodes_here, others)),
             dma((2,)),

time: 111 us -> 111 us (level)
  no operation moved by 1% of the time
where the time goes in v4:
time: 111 us; the launch traced here: 110 us
  Pallas kernels  109 us (98%)
  local copies, waits for them, and re-layouts  1.32 us (1%)
    pallas_call x1, Pallas kernels, local(): pl.pallas_call(functools.partial(kernel, cols, chunks), out_shape=pltpu.V...  109 us

profile of v4, /device:TPU:8, one launch (start us, length us, event | category | flops | bytes accessed | tf_op | source)
XLA Modules:
  0.0 110.2 jit_solution(871894683626312192)
XLA Ops:
  0.0 108.9 %shard_map.28 = bf16[4,256,1024]{2,1,0:T(8,128)(2,1)S(1)} custom-call(bf16[4,256,1024]{2,1,0:T(8,128)(2,1)} %x_in.1, bf16[3,4,4,128,256]{4,3,2,1,0:T(8,128)(2,1)} %t_in.1), custom_call_target="tpu_custom_call" | custom-call | tf_op jit(solution)/shard_map/pallas_call | solution.py:432
  108.9 1.3 %copy.4 = bf16[4,256,1024]{2,1,0:T(8,128)(2,1)} copy(bf16[4,256,1024]{2,1,0:T(8,128)(2,1)S(1)} %shard_map.28) | data formatting | bytes 4194304

commit v5 on v4

--- a/solution.py
+++ b/solution.py
@@ -10,9 +10,9 @@
 MESH = pl.DeviceIdType.MESH
 WIDTH = 256
 HELD_BACK = 4
-LAG_ONE, LAG_RELAY, LAG_FAR, LAG_MID, LAG_NEAR, LAG_END = 2, 4, 5, 8, 12, 10
+LAG_ONE, LAG_RELAY, LAG_FAR, LAG_MID, LAG_NEAR, LAG_END = 2, 4, 5, 8, 12, 12
 TO_TWO, FORWARD, TO_PAIR, TO_ACROSS, RELAY, PARTIAL, SUM_NEAR, SUM_FAR = range(8)
-ROW = {TO_TWO: 0, FORWARD: 1, TO_PAIR: 2, TO_ACROSS: 3, RELAY: 4, PARTIAL: 3, SUM_NEAR: 3, SUM_FAR: 4}
+ROW = {TO_TWO: 0, FORWARD: 1, TO_PAIR: 2, TO_ACROSS: 3, RELAY: 3, PARTIAL: 3, SUM_NEAR: 3, SUM_FAR: 3}
 
 
 def flip(i, bit):
@@ -25,8 +25,8 @@
 
 def kernel(
     cols, chunks, x_in, t_in, out_ref,
-    x, t, t_far, t_pass, t_sum, held, theirs, y1, pair, across, relayed, partial_out, partial_in, sums,
-    local_sem, send, recv, half_x, half_core, t_send, t_recv, far_send, far_recv, sum_send, sum_recv, spread_send, spread_recv,
+    x, t, t_far, t_pass, t_sum, held, theirs, y1, pair, come, partial_out, partial_in, sums,
+    local_sem, send, recv, far_sum, half_x, half_core, t_send, t_recv, far_send, far_recv, sum_send, sum_recv, spread_send, spread_recv,
 ):
     nodes_here = x_in.shape[0]
     last = nodes_here - 1
@@ -46,11 +46,6 @@
     by_across = flip(by_pair, 8)
     my_rows = pl.ds(my_col * rows, rows)
 
-    x_copy = pltpu.make_async_copy(x_in, x, local_sem.at[0])
-    x_copy.start()
-    t_copy = pltpu.make_async_copy(t_in, t.at[:, :, :, my_rows, :], local_sem.at[1])
-    t_copy.start()
-
     barrier = pltpu.get_barrier_semaphore()
     for k in range(1, cols):
         pl.semaphore_signal(barrier, inc=1, device_id={"col": (my_col + k) % cols}, device_id_type=MESH)
@@ -60,6 +55,14 @@
     @pl.when(is_mid)
     def _():
         pl.semaphore_signal(barrier, inc=1, device_id={"node": by_across}, device_id_type=MESH)
+
+    x_copy = pltpu.make_async_copy(x_in, x, local_sem.at[0])
+    x_copy.start()
+    t_copy = pltpu.make_async_copy(t_in, t.at[:, :, :, my_rows, :], local_sem.at[1])
+    t_copy.start()
+
+    @pl.when(is_mid)
+    def _():
         pl.semaphore_wait(barrier, 4 + cols - 1)
 
     @pl.when(is_end)
@@ -124,13 +127,14 @@
             TO_TWO: lambda: (held.at[u, 0], held.at[u, 1], by_two),
             FORWARD: lambda: (held.at[u], theirs.at[u], by_core),
             TO_PAIR: lambda: (y1.at[u], pair.at[u], by_pair),
-            TO_ACROSS: lambda: (y1.at[u], across.at[u], by_across),
-            RELAY: lambda: (pair.at[u], relayed.at[u], by_across),
+            TO_ACROSS: lambda: (y1.at[u], come.at[u, 0], by_across),
+            RELAY: lambda: (pair.at[u], come.at[u, 1], by_across),
             PARTIAL: lambda: (partial_out.at[u], partial_in.at[u], by_pair),
-            SUM_NEAR: lambda: (sums.at[0, u - plain], across.at[u], by_across),
-            SUM_FAR: lambda: (sums.at[1, u - plain], relayed.at[u], by_across),
+            SUM_NEAR: lambda: (sums.at[0, u - plain], come.at[u, 0], by_across),
+            SUM_FAR: lambda: (sums.at[1, u - plain], come.at[u, 1], by_across),
         }[kind]()
-        return remote(source, target, send.at[kind], recv.at[ROW[kind], u], {"node": device})
+        sem = far_sum.at[u - plain] if kind == SUM_FAR else recv.at[ROW[kind], u]
+        return remote(source, target, send.at[kind], sem, {"node": device})
 
     def sent(kind, source, target):
         remote(source, target, send.at[kind], recv.at[ROW[kind], 0], {"node": by_pair}).wait_send()
@@ -193,12 +197,16 @@
 
         def part(kind, target, device):
             remote(
-                y1.at[0, here, columns], target.at[0, here, columns],
+                y1.at[0, here, columns], target.at[here, columns],
                 send.at[kind], recv.at[ROW[kind], 0], {"node": device},
             ).start()
 
-        pl.when(is_mid)(lambda: part(TO_ACROSS, across, by_across))
-        pl.when(is_end)(lambda: part(TO_PAIR, pair, by_pair))
+        pl.when(is_mid)(lambda: part(TO_ACROSS, come.at[0, 0], by_across))
+        pl.when(is_end)(lambda: part(TO_PAIR, pair.at[0], by_pair))
+
+    def forward(u):
+        copy(TO_TWO, u).wait_recv()
+        copy(FORWARD, u).start()
 
     def first_unit():
         wait_rows(0, 0)
@@ -214,6 +222,8 @@
         for h in range(2):
             half_to_core(h).wait_recv()
             one_rows(rows_of(0), halves[h])
+        if chunks > 1:
+            forward(1)
         wait_rows(1, 0)
         for k in range(1, cols):
             one_rows(rows_of(k), whole)
@@ -229,8 +239,7 @@
         copy(TO_TWO, u).start()
 
     def stage_one(u):
-        copy(TO_TWO, u).wait_recv()
-        copy(FORWARD, u).start()
+        pl.when(u > (1 if chunks > 1 else 0))(lambda: forward(u))
         first(u, lambda m: wait_rows(1, m))
         m = u // chunks
         total = dot(t[1, m, one], held[u, 0])
@@ -297,17 +306,16 @@
 
             first(u, arrive)
             m = u // chunks
-            copy(TO_ACROSS, u).wait_recv()
-            copy(RELAY, u).wait_recv()
+            remote(come.at[u], come.at[u], send.at[RELAY], recv.at[ROW[RELAY], u], {"node": by_across}).wait_recv()
             start = 1 - two // 2
-            part = dot(t_far[m, 3 - two - start], across[u])
-            part += dot(t_far[m, flip(3 - two, 1) - start], relayed[u])
+            part = dot(t_far[m, 3 - two - start], come[u, 0])
+            part += dot(t_far[m, flip(3 - two, 1) - start], come[u, 1])
             part += dot(t_far[m, two - start], y1[u])
             partial_out[u] = part.astype(partial_out.dtype)
             copy(PARTIAL, u).start()
             total = own_part(u) + pair_part(u)
-            total += dot(t[2, m, 3 - two], across[u])
-            total += dot(t[2, m, flip(two, 2)], relayed[u])
+            total += dot(t[2, m, 3 - two], come[u, 0])
+            total += dot(t[2, m, flip(two, 2)], come[u, 1])
             store(u, total)
 
         @pl.when(u >= plain)
@@ -318,7 +326,7 @@
                 far(last).wait_recv()
 
             copy(SUM_FAR, u).wait_recv()
-            part = dot(t_far[last, 0], y1[u]) + relayed[u].astype(jnp.float32)
+            part = dot(t_far[last, 0], y1[u]) + come[u, 1].astype(jnp.float32)
             partial_out[u] = part.astype(partial_out.dtype)
             copy(PARTIAL, u).start()
 
@@ -327,7 +335,7 @@
         def _():
             total = own_part(u) + pair_part(u)
             copy(SUM_NEAR, u).wait_recv()
-            store(u, total + across[u].astype(jnp.float32))
+            store(u, total + come[u, 0].astype(jnp.float32))
 
     def stage_end(u):
         total = own_part(u)
@@ -389,11 +397,11 @@
     def _():
         early = pl.ds(0, plain)
         late = pl.ds(plain, units - plain)
-        sent(TO_ACROSS, y1.at[early], across.at[early])
-        sent(RELAY, pair.at[early], relayed.at[early])
+        sent(TO_ACROSS, y1.at[early], come.at[early, 0])
+        sent(RELAY, pair.at[early], come.at[early, 1])
         sent(PARTIAL, partial_out, partial_in)
-        sent(SUM_NEAR, sums.at[0], across.at[late])
-        sent(SUM_FAR, sums.at[1], across.at[late])
+        sent(SUM_NEAR, sums.at[0], come.at[late, 0])
+        sent(SUM_FAR, sums.at[1], come.at[late, 0])
         give().wait_send()
         give_on().wait_send()
         for k in range(1, cols):
@@ -444,14 +452,14 @@
             pltpu.VMEM((units, 2) + block, kind),
             pltpu.VMEM((units,) + block, kind),
             pltpu.VMEM((units,) + block, kind),
-            pltpu.VMEM((units,) + block, kind),
-            pltpu.VMEM((units,) + block, kind),
+            pltpu.VMEM((units, 2) + block, kind),
             pltpu.VMEM((units,) + block, kind),
             pltpu.VMEM((units,) + block, kind),
             pltpu.VMEM((2, chunks) + block, kind),
             dma((2,)),
             dma((8,)),
-            dma((5, units)),
+            dma((4, units)),
+            dma((chunks,)),
             dma((2, others)),
             dma((2,)),
             dma((3, others)),

time: 111 us -> 110 us (level)
  no operation moved by 1% of the time
where the time goes in v5:
time: 110 us
  Pallas kernels  109 us (99%)
  local copies, waits for them, and re-layouts  1.32 us (1%)
    pallas_call x1, Pallas kernels, local(): pl.pallas_call(functools.partial(kernel, cols, chunks), out_shape=pltpu.V...  109 us

profile of v5, /device:TPU:8, one launch (start us, length us, event | category | flops | bytes accessed | tf_op | source)
XLA Modules:
  0.0 110.1 jit_solution(14396771317622604034)
XLA Ops:
  0.0 108.8 %shard_map.28 = bf16[4,256,1024]{2,1,0:T(8,128)(2,1)S(1)} custom-call(bf16[4,256,1024]{2,1,0:T(8,128)(2,1)} %x_in.1, bf16[3,4,4,128,256]{4,3,2,1,0:T(8,128)(2,1)} %t_in.1), custom_call_target="tpu_custom_call" | custom-call | tf_op jit(solution)/shard_map/pallas_call | solution.py:440
  108.8 1.3 %copy.4 = bf16[4,256,1024]{2,1,0:T(8,128)(2,1)} copy(bf16[4,256,1024]{2,1,0:T(8,128)(2,1)S(1)} %shard_map.28) | data formatting | bytes 4194304

commit v6 on v5

--- a/solution.py
+++ b/solution.py
@@ -10,7 +10,7 @@
 MESH = pl.DeviceIdType.MESH
 WIDTH = 256
 HELD_BACK = 4
-LAG_ONE, LAG_RELAY, LAG_FAR, LAG_MID, LAG_NEAR, LAG_END = 2, 4, 5, 8, 12, 12
+LAG_ONE, LAG_RELAY, LAG_FAR, LAG_MID, LAG_NEAR, LAG_END = 2, 4, 5, 7, 11, 10
 TO_TWO, FORWARD, TO_PAIR, TO_ACROSS, RELAY, PARTIAL, SUM_NEAR, SUM_FAR = range(8)
 ROW = {TO_TWO: 0, FORWARD: 1, TO_PAIR: 2, TO_ACROSS: 3, RELAY: 3, PARTIAL: 3, SUM_NEAR: 3, SUM_FAR: 3}
 
@@ -362,9 +362,9 @@
             def _():
                 stage(u)
 
+        run(stage_relay, LAG_RELAY, is_mid)
         run(stage_mid, LAG_MID, is_mid)
         run(stage_near, LAG_NEAR, is_mid)
-        run(stage_relay, LAG_RELAY, is_mid)
         run(stage_one, LAG_ONE, start=1)
         @pl.when(s == LAG_ONE + 1)
         def _():

time: 110 us -> 110 us (level)
  no operation moved by 1% of the time
where the time goes in v6:
time: 110 us
  Pallas kernels  108 us (98%)
  local copies, waits for them, and re-layouts  1.32 us (1%)
    pallas_call x1, Pallas kernels, local(): pl.pallas_call(functools.partial(kernel, cols, chunks), out_shape=pltpu.V...  108 us

profile of v6, /device:TPU:8, one launch (start us, length us, event | category | flops | bytes accessed | tf_op | source)
XLA Modules:
  0.0 109.7 jit_solution(12232286401328066412)
XLA Ops:
  0.0 108.3 %shard_map.28 = bf16[4,256,1024]{2,1,0:T(8,128)(2,1)S(1)} custom-call(bf16[4,256,1024]{2,1,0:T(8,128)(2,1)} %x_in.1, bf16[3,4,4,128,256]{4,3,2,1,0:T(8,128)(2,1)} %t_in.1), custom_call_target="tpu_custom_call" | custom-call | tf_op jit(solution)/shard_map/pallas_call | solution.py:440
  108.4 1.3 %copy.4 = bf16[4,256,1024]{2,1,0:T(8,128)(2,1)} copy(bf16[4,256,1024]{2,1,0:T(8,128)(2,1)S(1)} %shard_map.28) | data formatting | bytes 4194304
